TPU v7x, 32 devices: a whole 2x2x4 slice. The times are simulated.
32 devices in a mesh: copy: 4 (over y, x), rows: 2 (over z_hi), cols: 2 (over core), slabs: 2 (over z_lo).
Axes of the slice: x: 2, y: 2, z: 4 (z_hi: 2, z_lo: 2; z = z_hi * 2 + z_lo), core: 2. Of those that a mesh axis runs over, the one named last changes fastest.
Arguments:
- density: float32 [128, 16, 128, 128], P(('copy', 'rows'), 'cols', 'slabs'), parts along dimension 0, may hold values from 0.2 to 1.8
- crowding: float32 [128, 16, 128, 128], P(('copy', 'rows'), 'cols', 'slabs'), parts along dimension 0, may hold values from 0.5 to 2
Outputs:
- potential: float32 [128, 16, 128, 128], P(('copy', 'rows'), 'cols', 'slabs'), parts along dimension 0
- density_end: float32 [128, 16, 128, 128], P(('copy', 'rows'), 'cols', 'slabs'), parts along dimension 0
There are 4 independent parts, one for each index of `copy`. A program takes and returns all parts, laid end to end along the dimension named above; each array names one. Nothing has to cross between parts.
All inputs are finite; a program needn't handle non-finite values.
Results may differ from a plain program's by a relative error of at most 0.00002.
Values sent between devices are 32-bit elements; how exact they have to be, the bound alone decides.
A program may use at most 128 MiB of HBM per device.

v0:
```python
import jax
import jax.numpy as jnp
from jax import lax
from jax.sharding import PartitionSpec as P

STEPS = 6


def padded_2(shard, sides, width):
    for axis, dim in sides:
        count, length = (lax.axis_size(axis), shard.shape[dim])
        up = [(i, (i + 1) % count) for i in range(count)]
        down = [(j, i) for i, j in up]
        last = lax.slice_in_dim(shard, length - width, length, axis=dim)
        initial = lax.slice_in_dim(shard, 0, width, axis=dim)
        before = lax.ppermute(last, axis, up)
        after = lax.ppermute(initial, axis, down)
        shard = jnp.concatenate([before, shard, after], axis=dim)
    return shard


def carried_in(value, axis, join, neutral):
    count, mine = (lax.axis_size(axis), lax.axis_index(axis))
    pieces = lax.all_gather(value, axis)
    so_far = jnp.full_like(value, 0) + jnp.asarray(neutral, value.dtype)

    def lap(position, so_far):
        longer = join(so_far, pieces[position])
        return jnp.where(position < mine, longer, so_far)

    return lax.fori_loop(0, count - 1, lap, so_far)


def strip_edges(values, dims):
    for dim in dims:
        values = lax.slice_in_dim(values, 1, values.shape[dim] - 1, axis=dim)
    return values


def neighbour(values, dim, start, dims):
    others = [other for other in dims if other != dim]
    values = strip_edges(values, others)
    return lax.slice_in_dim(values, start, start + values.shape[dim] - 2, axis=dim)


def one_step(padded, crowding):
    middle = strip_edges(padded, (0, 1, 2))
    lower = [neighbour(padded, dim, 0, (0, 1, 2)) for dim in (0, 1, 2)]
    upper = [neighbour(padded, dim, 2, (0, 1, 2)) for dim in (0, 1, 2)]
    spread = lower[0] + upper[0] + lower[1] + upper[1] + lower[2] + upper[2] - 6.0 * middle
    return middle + 0.1 * spread + 0.2 * middle * (1.0 - middle * crowding)


def per_device(density, crowding):
    for step in range(STEPS):
        padded = padded_2(density, (("rows", 0), ("cols", 1), ("slabs", 2)), 1)
        density = one_step(padded, crowding)
    here = jnp.cumsum(density, axis=1)
    total = lax.slice_in_dim(here, here.shape[1] - 1, here.shape[1], axis=1)

    def add_pair(earlier_total, later_total):
        return earlier_total + later_total

    below = carried_in(total, "cols", add_pair, jnp.zeros_like(total))
    potential = (here + below) / (density.shape[1] * lax.axis_size("cols"))
    return (potential, density)


def solution(mesh):
    return jax.shard_map(
        per_device,
        mesh=mesh,
        in_specs=(
            P(("copy", "rows"), "cols", "slabs", None),
            P(("copy", "rows"), "cols", "slabs", None),
        ),
        out_specs=(
            P(("copy", "rows"), "cols", "slabs", None),
            P(("copy", "rows"), "cols", "slabs", None),
        ),
        check_vma=False,
    )
```

profile of v0, /device:TPU:0, one launch (start us, length us, event | category | flops | bytes accessed | tf_op | source)
XLA Modules:
  0.0 354.1 jit_solution(10507626476265467478)
XLA Ops:
  8.3 4.1 %collective-permute-start = (f32[1,8,64,128]{3,2,1,0:T(8,128)S(1)}, f32[1,8,64,128]{3,2,1,0:T(8,128)S(1)}, u32[]{:S(2)}, u32[]{:S(2)}) collective-permute-start(f32[1,8,64,128]{3,2,1,0:T(8,128)S(1)} %get-tuple-element.54), channel_id=1, source_target_pairs={{0,4},{4,0},{1,5},{5,1},{2,6},{6,2},{3,7},{7,3},{8,12},{12,8},{9,1... | collective-permute-start | bytes 786440 | tf_op jit(solution)/shard_map/ppermute | solution.py:16
  12.5 18.3 %collective-permute-done = f32[1,8,64,128]{3,2,1,0:T(8,128)S(1)} collective-permute-done((f32[1,8,64,128]{3,2,1,0:T(8,128)S(1)}, f32[1,8,64,128]{3,2,1,0:T(8,128)S(1)}, u32[]{:S(2)}, u32[]{:S(2)}) %collective-permute-start) | collective-permute-done | bytes 262176 | tf_op jit(solution)/shard_map/ppermute | solution.py:16
  30.8 2.5 constant_dynamic-update-slice_fusion.1
  41.0 4.1 %collective-permute-done.4 = f32[18,10,1,128]{3,0,2,1:T(8,128)S(1)} collective-permute-done((f32[18,10,1,128]{3,0,2,1:T(8,128)S(1)}, f32[18,10,1,128]{3,0,2,1:T(8,128)S(1)}, u32[]{:S(2)}, u32[]{:S(2)}) %collective-permute-start.4) | collective-permute-done | bytes 92192 | tf_op jit(solution)/shard_map/ppermute | solution.py:16
  47.0 17.4 %fusion.49 = f32[16,8,64,128]{3,2,1,0:T(8,128)S(1)} fusion(f32[16,8,64,128]{3,2,1,0:T(8,128)} %param.2, f32[18,10,1,128]{3,2,1,0:T(1,128)S(1)} %copy.26, f32[18,1,64,128]{3,2,1,0:T(8,128)S(1)} %collective-permute-done.3, f32[18,8,64,128]{3,2,1,0:T(8,128)} %copy-done.5, f32[18,1,64,128]{3,2,1,0:T(8,128)S(1)} %collective-permute-done.2, ...), kind=kLoop, calls=%fused_computation.140 | loop fusion | flops 25165824 | bytes 19189760 | tf_op jit(solution)/shard_map/add | solution.py:51
  64.4 2.4 collective-permute-start.6
  67.4 17.7 %collective-permute-done.6 = f32[1,8,64,128]{3,2,1,0:T(8,128)S(1)} collective-permute-done((f32[1,8,64,128]{3,2,1,0:T(8,128)S(1)}, f32[1,8,64,128]{3,2,1,0:T(8,128)S(1)}, u32[]{:S(2)}, u32[]{:S(2)}) %collective-permute-start.6) | collective-permute-done | bytes 262176 | tf_op jit(solution)/shard_map/ppermute | solution.py:16
  85.1 4.6 %collective-permute-done.7 = f32[1,8,64,128]{3,2,1,0:T(8,128)S(1)} collective-permute-done((f32[1,8,64,128]{3,2,1,0:T(8,128)S(1)}, f32[1,8,64,128]{3,2,1,0:T(8,128)S(1)}, u32[]{:S(2)}, u32[]{:S(2)}) %collective-permute-start.7) | collective-permute-done | bytes 262176 | tf_op jit(solution)/shard_map/ppermute | solution.py:17
  95.1 4.1 %collective-permute-done.10 = f32[18,10,1,128]{3,0,2,1:T(8,128)S(1)} collective-permute-done((f32[18,10,1,128]{3,0,2,1:T(8,128)S(1)}, f32[18,10,1,128]{3,0,2,1:T(8,128)S(1)}, u32[]{:S(2)}, u32[]{:S(2)}) %collective-permute-start.10) | collective-permute-done | bytes 92192 | tf_op jit(solution)/shard_map/ppermute | solution.py:16
  101.1 18.8 %fusion.40 = f32[16,8,64,128]{3,2,1,0:T(8,128)S(1)} fusion(f32[16,8,64,128]{3,2,1,0:T(8,128)} %copy-done.4, f32[18,10,1,128]{3,2,1,0:T(1,128)S(1)} %copy.30, f32[18,1,64,128]{3,2,1,0:T(8,128)S(1)} %collective-permute-done.9, f32[18,1,64,128]{3,2,1,0:T(8,128)S(1)} %collective-permute-done.8, f32[1,8,64,128]{3,2,1,0:T(8,128)S(1)} %collective-permute-done.7, ...), kind=kLoop, calls=%fused_computation.113 | loop fusion | flops 33554432 | bytes 14471168 | tf_op jit(solution)/shard_map/add | solution.py:51
  122.9 17.7 %collective-permute-done.12 = f32[1,8,64,128]{3,2,1,0:T(8,128)S(1)} collective-permute-done((f32[1,8,64,128]{3,2,1,0:T(8,128)S(1)}, f32[1,8,64,128]{3,2,1,0:T(8,128)S(1)}, u32[]{:S(2)}, u32[]{:S(2)}) %collective-permute-start.12) | collective-permute-done | bytes 262176 | tf_op jit(solution)/shard_map/ppermute | solution.py:16
  140.6 4.6 %collective-permute-done.13 = f32[1,8,64,128]{3,2,1,0:T(8,128)S(1)} collective-permute-done((f32[1,8,64,128]{3,2,1,0:T(8,128)S(1)}, f32[1,8,64,128]{3,2,1,0:T(8,128)S(1)}, u32[]{:S(2)}, u32[]{:S(2)}) %collective-permute-start.13) | collective-permute-done | bytes 262176 | tf_op jit(solution)/shard_map/ppermute | solution.py:17
  150.6 4.1 %collective-permute-done.16 = f32[18,10,1,128]{3,0,2,1:T(8,128)S(1)} collective-permute-done((f32[18,10,1,128]{3,0,2,1:T(8,128)S(1)}, f32[18,10,1,128]{3,0,2,1:T(8,128)S(1)}, u32[]{:S(2)}, u32[]{:S(2)}) %collective-permute-start.16) | collective-permute-done | bytes 92192 | tf_op jit(solution)/shard_map/ppermute | solution.py:16
  156.6 12.8 %fusion.31 = f32[16,8,64,128]{3,2,1,0:T(8,128)} fusion(f32[16,8,64,128]{3,2,1,0:T(8,128)S(1)} %fusion.40, f32[18,10,1,128]{3,2,1,0:T(1,128)S(1)} %copy.34, f32[18,1,64,128]{3,2,1,0:T(8,128)S(1)} %collective-permute-done.15, f32[18,1,64,128]{3,2,1,0:T(8,128)S(1)} %collective-permute-done.14, f32[1,8,64,128]{3,2,1,0:T(8,128)S(1)} %collective-permute-done.13, ...), kind=kLoop, calls=%fused_computation.86 | loop fusion | flops 33554432 | bytes 14471168 | tf_op jit(solution)/shard_map/add | solution.py:51
  170.6 2.4 collective-permute-start.18
  173.6 17.7 %collective-permute-done.18 = f32[1,8,64,128]{3,2,1,0:T(8,128)S(1)} collective-permute-done((f32[1,8,64,128]{3,2,1,0:T(8,128)S(1)}, f32[1,8,64,128]{3,2,1,0:T(8,128)S(1)}, u32[]{:S(2)}, u32[]{:S(2)}) %collective-permute-start.18) | collective-permute-done | bytes 262176 | tf_op jit(solution)/shard_map/ppermute | solution.py:16
  191.3 4.6 %collective-permute-done.19 = f32[1,8,64,128]{3,2,1,0:T(8,128)S(1)} collective-permute-done((f32[1,8,64,128]{3,2,1,0:T(8,128)S(1)}, f32[1,8,64,128]{3,2,1,0:T(8,128)S(1)}, u32[]{:S(2)}, u32[]{:S(2)}) %collective-permute-start.19) | collective-permute-done | bytes 262176 | tf_op jit(solution)/shard_map/ppermute | solution.py:17
  202.5 4.1 %collective-permute-done.22 = f32[18,10,1,128]{3,0,2,1:T(8,128)S(1)} collective-permute-done((f32[18,10,1,128]{3,0,2,1:T(8,128)S(1)}, f32[18,10,1,128]{3,0,2,1:T(8,128)S(1)}, u32[]{:S(2)}, u32[]{:S(2)}) %collective-permute-start.22) | collective-permute-done | bytes 92192 | tf_op jit(solution)/shard_map/ppermute | solution.py:16
  208.5 12.8 %fusion.22 = f32[16,8,64,128]{3,2,1,0:T(8,128)} fusion(f32[16,8,64,128]{3,2,1,0:T(8,128)S(1)} %copy-done.1, f32[18,10,1,128]{3,2,1,0:T(1,128)S(1)} %copy.38, f32[18,1,64,128]{3,2,1,0:T(8,128)S(1)} %collective-permute-done.21, f32[18,1,64,128]{3,2,1,0:T(8,128)S(1)} %collective-permute-done.20, f32[1,8,64,128]{3,2,1,0:T(8,128)S(1)} %collective-permute-done.19, ...), kind=kLoop, calls=%fused_computation.59 | loop fusion | flops 33554432 | bytes 14471168 | tf_op jit(solution)/shard_map/add | solution.py:51
  222.5 2.4 collective-permute-start.24
  225.5 17.7 %collective-permute-done.24 = f32[1,8,64,128]{3,2,1,0:T(8,128)S(1)} collective-permute-done((f32[1,8,64,128]{3,2,1,0:T(8,128)S(1)}, f32[1,8,64,128]{3,2,1,0:T(8,128)S(1)}, u32[]{:S(2)}, u32[]{:S(2)}) %collective-permute-start.24) | collective-permute-done | bytes 262176 | tf_op jit(solution)/shard_map/ppermute | solution.py:16
  243.2 4.6 %collective-permute-done.25 = f32[1,8,64,128]{3,2,1,0:T(8,128)S(1)} collective-permute-done((f32[1,8,64,128]{3,2,1,0:T(8,128)S(1)}, f32[1,8,64,128]{3,2,1,0:T(8,128)S(1)}, u32[]{:S(2)}, u32[]{:S(2)}) %collective-permute-start.25) | collective-permute-done | bytes 262176 | tf_op jit(solution)/shard_map/ppermute | solution.py:17
  254.4 4.1 %collective-permute-done.28 = f32[18,10,1,128]{3,0,2,1:T(8,128)S(1)} collective-permute-done((f32[18,10,1,128]{3,0,2,1:T(8,128)S(1)}, f32[18,10,1,128]{3,0,2,1:T(8,128)S(1)}, u32[]{:S(2)}, u32[]{:S(2)}) %collective-permute-start.28) | collective-permute-done | bytes 92192 | tf_op jit(solution)/shard_map/ppermute | solution.py:16
  260.3 12.8 %fusion.13 = f32[16,8,64,128]{3,2,1,0:T(8,128)} fusion(f32[16,8,64,128]{3,2,1,0:T(8,128)S(1)} %copy-done.2, f32[18,10,1,128]{3,2,1,0:T(1,128)S(1)} %copy.42, f32[18,1,64,128]{3,2,1,0:T(8,128)S(1)} %collective-permute-done.27, f32[18,1,64,128]{3,2,1,0:T(8,128)S(1)} %collective-permute-done.26, f32[1,8,64,128]{3,2,1,0:T(8,128)S(1)} %collective-permute-done.25, ...), kind=kLoop, calls=%fused_computation.32 | loop fusion | flops 33554432 | bytes 14471168 | tf_op jit(solution)/shard_map/add | solution.py:51
  274.4 2.4 collective-permute-start.30
  277.4 17.7 %collective-permute-done.30 = f32[1,8,64,128]{3,2,1,0:T(8,128)S(1)} collective-permute-done((f32[1,8,64,128]{3,2,1,0:T(8,128)S(1)}, f32[1,8,64,128]{3,2,1,0:T(8,128)S(1)}, u32[]{:S(2)}, u32[]{:S(2)}) %collective-permute-start.30) | collective-permute-done | bytes 262176 | tf_op jit(solution)/shard_map/ppermute | solution.py:16
  295.1 4.6 %collective-permute-done.31 = f32[1,8,64,128]{3,2,1,0:T(8,128)S(1)} collective-permute-done((f32[1,8,64,128]{3,2,1,0:T(8,128)S(1)}, f32[1,8,64,128]{3,2,1,0:T(8,128)S(1)}, u32[]{:S(2)}, u32[]{:S(2)}) %collective-permute-start.31) | collective-permute-done | bytes 262176 | tf_op jit(solution)/shard_map/ppermute | solution.py:17
  306.2 4.1 %collective-permute-done.34 = f32[18,10,1,128]{3,0,2,1:T(8,128)S(1)} collective-permute-done((f32[18,10,1,128]{3,0,2,1:T(8,128)S(1)}, f32[18,10,1,128]{3,0,2,1:T(8,128)S(1)}, u32[]{:S(2)}, u32[]{:S(2)}) %collective-permute-start.34) | collective-permute-done | bytes 92192 | tf_op jit(solution)/shard_map/ppermute | solution.py:16
  312.2 12.8 %fusion.4 = f32[16,8,64,128]{3,2,1,0:T(8,128)} fusion(f32[16,8,64,128]{3,2,1,0:T(8,128)S(1)} %copy-done.3, f32[18,10,1,128]{3,2,1,0:T(1,128)S(1)} %copy.46, f32[18,1,64,128]{3,2,1,0:T(8,128)S(1)} %collective-permute-done.33, f32[18,1,64,128]{3,2,1,0:T(8,128)S(1)} %collective-permute-done.32, f32[1,8,64,128]{3,2,1,0:T(8,128)S(1)} %collective-permute-done.31, ...), kind=kLoop, calls=%fused_computation.5 | loop fusion | flops 33554432 | bytes 14471168 | tf_op jit(solution)/shard_map/add | solution.py:51
  325.0 2.7 fusion.62
  330.6 10.4 %all-gather.3.cloned.1.call-done = f32[32,1,64,128]{3,2,1,0:T(8,128)} async-done(((f32[16,1,64,128]{3,2,1,0:T(8,128)}), f32[32,1,64,128]{3,2,1,0:T(8,128)}) %all-gather.3.cloned.1.call-update) | async-done | bytes 1048592 | tf_op jit(solution)/shard_map/all_gather | solution.py:24
  342.1 5.2 %add_multiply_fusion = f32[16,8,64,128]{3,2,1,0:T(8,128)} fusion(f32[16,8,64,128]{3,2,1,0:T(8,128)} %copy-done.6, f32[16,64,128]{2,1,0:T(8,128)S(1)} %fusion.54), kind=kLoop, calls=%fused_computation.154 | loop fusion | flops 2097152 | bytes 8912896 | tf_op jit(solution)/shard_map/div | solution.py:65
  (112 shorter events, 63.2 us)
Async XLA Ops:
  7.2 333.8 %all-gather.3.cloned.1.call-start = ((), (), s32[]{:S(2)}) async-start(), calls=%async_computation | async-start | bytes 1572864 | tf_op jit(solution)/shard_map/all_gather | solution.py:24
  8.3 22.5 %collective-permute-start = (f32[1,8,64,128]{3,2,1,0:T(8,128)S(1)}, f32[1,8,64,128]{3,2,1,0:T(8,128)S(1)}, u32[]{:S(2)}, u32[]{:S(2)}) collective-permute-start(f32[1,8,64,128]{3,2,1,0:T(8,128)S(1)} %get-tuple-element.54), channel_id=1, source_target_pairs={{0,4},{4,0},{1,5},{5,1},{2,6},{6,2},{3,7},{7,3},{8,12},{12,8},{9,1... | collective-permute-start | bytes 786440 | tf_op jit(solution)/shard_map/ppermute | solution.py:16
  12.4 23.2 %collective-permute-start.1 = (f32[1,8,64,128]{3,2,1,0:T(8,128)S(1)}, f32[1,8,64,128]{3,2,1,0:T(8,128)S(1)}, u32[]{:S(2)}, u32[]{:S(2)}) collective-permute-start(f32[1,8,64,128]{3,2,1,0:T(8,128)S(1)} %get-tuple-element.53), channel_id=1, source_target_pairs={{4,0},{0,4},{5,1},{1,5},{6,2},{2,6},{7,3},{3,7},{12,8},{8,12},{13,... | collective-permute-start | bytes 786440 | tf_op jit(solution)/shard_map/ppermute | solution.py:17
  35.8 2.8 collective-permute-start.3
  38.8 6.3 %collective-permute-start.4 = (f32[18,10,1,128]{3,0,2,1:T(8,128)S(1)}, f32[18,10,1,128]{3,0,2,1:T(8,128)S(1)}, u32[]{:S(2)}, u32[]{:S(2)}) collective-permute-start(f32[18,10,1,128]{3,0,2,1:T(8,128)S(1)} %copy.23), channel_id=1, source_target_pairs={{0,1},{1,0},{2,3},{3,2},{4,5},{5,4},{6,7},{7,6},{8,9},{9,8},{10,11... | collective-permute-start | bytes 276488 | tf_op jit(solution)/shard_map/ppermute | solution.py:16
  39.6 7.3 %collective-permute-start.5 = (f32[18,10,1,128]{3,0,2,1:T(8,128)S(1)}, f32[18,10,1,128]{3,0,2,1:T(8,128)S(1)}, u32[]{:S(2)}, u32[]{:S(2)}) collective-permute-start(f32[18,10,1,128]{3,0,2,1:T(8,128)S(1)} %copy.25), channel_id=1, source_target_pairs={{1,0},{0,1},{3,2},{2,3},{5,4},{4,5},{7,6},{6,7},{9,8},{8,9},{11,10... | collective-permute-start | bytes 276488 | tf_op jit(solution)/shard_map/ppermute | solution.py:17
  64.4 20.7 %collective-permute-start.6 = (f32[1,8,64,128]{3,2,1,0:T(8,128)S(1)}, f32[1,8,64,128]{3,2,1,0:T(8,128)S(1)}, u32[]{:S(2)}, u32[]{:S(2)}) collective-permute-start(f32[1,8,64,128]{3,2,1,0:T(8,128)S(1)} %get-tuple-element.51), channel_id=1, source_target_pairs={{0,4},{4,0},{1,5},{5,1},{2,6},{6,2},{3,7},{7,3},{8,12},{12,8},{9,1... | collective-permute-start | bytes 786440 | tf_op jit(solution)/shard_map/ppermute | solution.py:16
  66.8 22.9 %collective-permute-start.7 = (f32[1,8,64,128]{3,2,1,0:T(8,128)S(1)}, f32[1,8,64,128]{3,2,1,0:T(8,128)S(1)}, u32[]{:S(2)}, u32[]{:S(2)}) collective-permute-start(f32[1,8,64,128]{3,2,1,0:T(8,128)S(1)} %get-tuple-element.52), channel_id=1, source_target_pairs={{4,0},{0,4},{5,1},{1,5},{6,2},{2,6},{7,3},{3,7},{12,8},{8,12},{13,... | collective-permute-start | bytes 786440 | tf_op jit(solution)/shard_map/ppermute | solution.py:17
  89.8 2.1 collective-permute-start.8
  89.9 2.8 collective-permute-start.9
  92.9 6.3 %collective-permute-start.10 = (f32[18,10,1,128]{3,0,2,1:T(8,128)S(1)}, f32[18,10,1,128]{3,0,2,1:T(8,128)S(1)}, u32[]{:S(2)}, u32[]{:S(2)}) collective-permute-start(f32[18,10,1,128]{3,0,2,1:T(8,128)S(1)} %copy.27), channel_id=1, source_target_pairs={{0,1},{1,0},{2,3},{3,2},{4,5},{5,4},{6,7},{7,6},{8,9},{9,8},{10,11... | collective-permute-start | bytes 276488 | tf_op jit(solution)/shard_map/ppermute | solution.py:16
  93.7 7.3 %collective-permute-start.11 = (f32[18,10,1,128]{3,0,2,1:T(8,128)S(1)}, f32[18,10,1,128]{3,0,2,1:T(8,128)S(1)}, u32[]{:S(2)}, u32[]{:S(2)}) collective-permute-start(f32[18,10,1,128]{3,0,2,1:T(8,128)S(1)} %copy.29), channel_id=1, source_target_pairs={{1,0},{0,1},{3,2},{2,3},{5,4},{4,5},{7,6},{6,7},{9,8},{8,9},{11,10... | collective-permute-start | bytes 276488 | tf_op jit(solution)/shard_map/ppermute | solution.py:17
  119.9 20.7 %collective-permute-start.12 = (f32[1,8,64,128]{3,2,1,0:T(8,128)S(1)}, f32[1,8,64,128]{3,2,1,0:T(8,128)S(1)}, u32[]{:S(2)}, u32[]{:S(2)}) collective-permute-start(f32[1,8,64,128]{3,2,1,0:T(8,128)S(1)} %get-tuple-element.49), channel_id=1, source_target_pairs={{0,4},{4,0},{1,5},{5,1},{2,6},{6,2},{3,7},{7,3},{8,12},{12,8},{9,1... | collective-permute-start | bytes 786440 | tf_op jit(solution)/shard_map/ppermute | solution.py:16
  122.4 22.9 %collective-permute-start.13 = (f32[1,8,64,128]{3,2,1,0:T(8,128)S(1)}, f32[1,8,64,128]{3,2,1,0:T(8,128)S(1)}, u32[]{:S(2)}, u32[]{:S(2)}) collective-permute-start(f32[1,8,64,128]{3,2,1,0:T(8,128)S(1)} %get-tuple-element.50), channel_id=1, source_target_pairs={{4,0},{0,4},{5,1},{1,5},{6,2},{2,6},{7,3},{3,7},{12,8},{8,12},{13,... | collective-permute-start | bytes 786440 | tf_op jit(solution)/shard_map/ppermute | solution.py:17
  145.5 2.8 collective-permute-start.15
  148.4 6.3 %collective-permute-start.16 = (f32[18,10,1,128]{3,0,2,1:T(8,128)S(1)}, f32[18,10,1,128]{3,0,2,1:T(8,128)S(1)}, u32[]{:S(2)}, u32[]{:S(2)}) collective-permute-start(f32[18,10,1,128]{3,0,2,1:T(8,128)S(1)} %copy.31), channel_id=1, source_target_pairs={{0,1},{1,0},{2,3},{3,2},{4,5},{5,4},{6,7},{7,6},{8,9},{9,8},{10,11... | collective-permute-start | bytes 276488 | tf_op jit(solution)/shard_map/ppermute | solution.py:16
  149.2 7.3 %collective-permute-start.17 = (f32[18,10,1,128]{3,0,2,1:T(8,128)S(1)}, f32[18,10,1,128]{3,0,2,1:T(8,128)S(1)}, u32[]{:S(2)}, u32[]{:S(2)}) collective-permute-start(f32[18,10,1,128]{3,0,2,1:T(8,128)S(1)} %copy.33), channel_id=1, source_target_pairs={{1,0},{0,1},{3,2},{2,3},{5,4},{4,5},{7,6},{6,7},{9,8},{8,9},{11,10... | collective-permute-start | bytes 276488 | tf_op jit(solution)/shard_map/ppermute | solution.py:17
  170.6 20.7 %collective-permute-start.18 = (f32[1,8,64,128]{3,2,1,0:T(8,128)S(1)}, f32[1,8,64,128]{3,2,1,0:T(8,128)S(1)}, u32[]{:S(2)}, u32[]{:S(2)}) collective-permute-start(f32[1,8,64,128]{3,2,1,0:T(8,128)S(1)} %get-tuple-element.47), channel_id=1, source_target_pairs={{0,4},{4,0},{1,5},{5,1},{2,6},{6,2},{3,7},{7,3},{8,12},{12,8},{9,1... | collective-permute-start | bytes 786440 | tf_op jit(solution)/shard_map/ppermute | solution.py:16
  173.1 22.9 %collective-permute-start.19 = (f32[1,8,64,128]{3,2,1,0:T(8,128)S(1)}, f32[1,8,64,128]{3,2,1,0:T(8,128)S(1)}, u32[]{:S(2)}, u32[]{:S(2)}) collective-permute-start(f32[1,8,64,128]{3,2,1,0:T(8,128)S(1)} %get-tuple-element.48), channel_id=1, source_target_pairs={{4,0},{0,4},{5,1},{1,5},{6,2},{2,6},{7,3},{3,7},{12,8},{8,12},{13,... | collective-permute-start | bytes 786440 | tf_op jit(solution)/shard_map/ppermute | solution.py:17
  197.3 2.8 collective-permute-start.21
  200.3 6.3 %collective-permute-start.22 = (f32[18,10,1,128]{3,0,2,1:T(8,128)S(1)}, f32[18,10,1,128]{3,0,2,1:T(8,128)S(1)}, u32[]{:S(2)}, u32[]{:S(2)}) collective-permute-start(f32[18,10,1,128]{3,0,2,1:T(8,128)S(1)} %copy.35), channel_id=1, source_target_pairs={{0,1},{1,0},{2,3},{3,2},{4,5},{5,4},{6,7},{7,6},{8,9},{9,8},{10,11... | collective-permute-start | bytes 276488 | tf_op jit(solution)/shard_map/ppermute | solution.py:16
  201.1 7.3 %collective-permute-start.23 = (f32[18,10,1,128]{3,0,2,1:T(8,128)S(1)}, f32[18,10,1,128]{3,0,2,1:T(8,128)S(1)}, u32[]{:S(2)}, u32[]{:S(2)}) collective-permute-start(f32[18,10,1,128]{3,0,2,1:T(8,128)S(1)} %copy.37), channel_id=1, source_target_pairs={{1,0},{0,1},{3,2},{2,3},{5,4},{4,5},{7,6},{6,7},{9,8},{8,9},{11,10... | collective-permute-start | bytes 276488 | tf_op jit(solution)/shard_map/ppermute | solution.py:17
  222.5 20.7 %collective-permute-start.24 = (f32[1,8,64,128]{3,2,1,0:T(8,128)S(1)}, f32[1,8,64,128]{3,2,1,0:T(8,128)S(1)}, u32[]{:S(2)}, u32[]{:S(2)}) collective-permute-start(f32[1,8,64,128]{3,2,1,0:T(8,128)S(1)} %get-tuple-element.45), channel_id=1, source_target_pairs={{0,4},{4,0},{1,5},{5,1},{2,6},{6,2},{3,7},{7,3},{8,12},{12,8},{9,1... | collective-permute-start | bytes 786440 | tf_op jit(solution)/shard_map/ppermute | solution.py:16
  224.9 22.9 %collective-permute-start.25 = (f32[1,8,64,128]{3,2,1,0:T(8,128)S(1)}, f32[1,8,64,128]{3,2,1,0:T(8,128)S(1)}, u32[]{:S(2)}, u32[]{:S(2)}) collective-permute-start(f32[1,8,64,128]{3,2,1,0:T(8,128)S(1)} %get-tuple-element.46), channel_id=1, source_target_pairs={{4,0},{0,4},{5,1},{1,5},{6,2},{2,6},{7,3},{3,7},{12,8},{8,12},{13,... | collective-permute-start | bytes 786440 | tf_op jit(solution)/shard_map/ppermute | solution.py:17
  249.2 2.8 collective-permute-start.27
  252.2 6.3 %collective-permute-start.28 = (f32[18,10,1,128]{3,0,2,1:T(8,128)S(1)}, f32[18,10,1,128]{3,0,2,1:T(8,128)S(1)}, u32[]{:S(2)}, u32[]{:S(2)}) collective-permute-start(f32[18,10,1,128]{3,0,2,1:T(8,128)S(1)} %copy.39), channel_id=1, source_target_pairs={{0,1},{1,0},{2,3},{3,2},{4,5},{5,4},{6,7},{7,6},{8,9},{9,8},{10,11... | collective-permute-start | bytes 276488 | tf_op jit(solution)/shard_map/ppermute | solution.py:16
  253.0 7.3 %collective-permute-start.29 = (f32[18,10,1,128]{3,0,2,1:T(8,128)S(1)}, f32[18,10,1,128]{3,0,2,1:T(8,128)S(1)}, u32[]{:S(2)}, u32[]{:S(2)}) collective-permute-start(f32[18,10,1,128]{3,0,2,1:T(8,128)S(1)} %copy.41), channel_id=1, source_target_pairs={{1,0},{0,1},{3,2},{2,3},{5,4},{4,5},{7,6},{6,7},{9,8},{8,9},{11,10... | collective-permute-start | bytes 276488 | tf_op jit(solution)/shard_map/ppermute | solution.py:17
  274.4 20.7 %collective-permute-start.30 = (f32[1,8,64,128]{3,2,1,0:T(8,128)S(1)}, f32[1,8,64,128]{3,2,1,0:T(8,128)S(1)}, u32[]{:S(2)}, u32[]{:S(2)}) collective-permute-start(f32[1,8,64,128]{3,2,1,0:T(8,128)S(1)} %get-tuple-element.43), channel_id=1, source_target_pairs={{0,4},{4,0},{1,5},{5,1},{2,6},{6,2},{3,7},{7,3},{8,12},{12,8},{9,1... | collective-permute-start | bytes 786440 | tf_op jit(solution)/shard_map/ppermute | solution.py:16
  276.8 22.9 %collective-permute-start.31 = (f32[1,8,64,128]{3,2,1,0:T(8,128)S(1)}, f32[1,8,64,128]{3,2,1,0:T(8,128)S(1)}, u32[]{:S(2)}, u32[]{:S(2)}) collective-permute-start(f32[1,8,64,128]{3,2,1,0:T(8,128)S(1)} %get-tuple-element.44), channel_id=1, source_target_pairs={{4,0},{0,4},{5,1},{1,5},{6,2},{2,6},{7,3},{3,7},{12,8},{8,12},{13,... | collective-permute-start | bytes 786440 | tf_op jit(solution)/shard_map/ppermute | solution.py:17
  301.1 2.8 collective-permute-start.33
  304.1 6.3 %collective-permute-start.34 = (f32[18,10,1,128]{3,0,2,1:T(8,128)S(1)}, f32[18,10,1,128]{3,0,2,1:T(8,128)S(1)}, u32[]{:S(2)}, u32[]{:S(2)}) collective-permute-start(f32[18,10,1,128]{3,0,2,1:T(8,128)S(1)} %copy.43), channel_id=1, source_target_pairs={{0,1},{1,0},{2,3},{3,2},{4,5},{5,4},{6,7},{7,6},{8,9},{9,8},{10,11... | collective-permute-start | bytes 276488 | tf_op jit(solution)/shard_map/ppermute | solution.py:16
  304.9 7.3 %collective-permute-start.35 = (f32[18,10,1,128]{3,0,2,1:T(8,128)S(1)}, f32[18,10,1,128]{3,0,2,1:T(8,128)S(1)}, u32[]{:S(2)}, u32[]{:S(2)}) collective-permute-start(f32[18,10,1,128]{3,0,2,1:T(8,128)S(1)} %copy.45), channel_id=1, source_target_pairs={{1,0},{0,1},{3,2},{2,3},{5,4},{4,5},{7,6},{6,7},{9,8},{8,9},{11,10... | collective-permute-start | bytes 276488 | tf_op jit(solution)/shard_map/ppermute | solution.py:17
  (12 other events, 155.7 us)
Sparse Core Ops, SparseCore 0:
  330.7 10.1 all-gather.2
where the time goes:
time: 354 us
  waiting for transfers between devices  191 us (54%)
  other arithmetic  101 us (29%)
  starting transfers between devices  35.5 us (10%)
  between operations  14.4 us (4%)
  local copies, waits for them, and re-layouts  11.6 us (3%)
    ppermute x18, waiting for transfers between devices, padded_2(): before = lax.ppermute(last, axis, up)  140 us
    add x6, other arithmetic, one_step(): return middle + 0.1 * spread + 0.2 * middle * (1.0 - middle * crowding)  87.5 us
    ppermute x18, waiting for transfers between devices, padded_2(): after = lax.ppermute(initial, axis, down)  40.7 us
    ppermute x18, starting transfers between devices, padded_2(): before = lax.ppermute(last, axis, up)  21.4 us
    ppermute x18, starting transfers between devices, padded_2(): after = lax.ppermute(initial, axis, down)  14.1 us
    all_gather x1, waiting for transfers between devices, carried_in(): pieces = lax.all_gather(value, axis)  10.4 us
  transfers between devices with their start and end apart: 37, of which 37 were waited for; matrix products, arithmetic and copies ran while one was open for 1% of the time, Pallas kernels for 0%

commit v1 on v0

v1 whole, which is shorter than its diff:
```python
import functools

import jax
import jax.numpy as jnp
from jax import lax
from jax.experimental import pallas as pl
from jax.experimental.pallas import tpu as pltpu
from jax.sharding import PartitionSpec as P

STEPS = 6
MESH = pl.DeviceIdType.MESH
PAD = 8


def kernel(shape, counts, dens, crow, pot_out, end_out, X, C, PT, KS, KR, TS, TR,
           js, jr, is_, ir, ks, kr, ts, tr, ls):
    J, I, K, S = shape
    n_rows, n_cols, n_slabs = counts
    cells = I * n_cols
    inner = pl.ds(PAD, K)

    def ring(axis, count, offset):
        return {axis: lax.rem(lax.axis_index(axis) + (offset + count), count)}

    load_d = pltpu.make_async_copy(dens, X.at[0, pl.ds(1, J), pl.ds(1, I), inner, :], ls.at[0])
    load_c = pltpu.make_async_copy(crow, C, ls.at[1])
    load_d.start()
    load_c.start()

    barrier = pltpu.get_barrier_semaphore()
    greeted = [ring("rows", n_rows, o) for o in (-1, 1)]
    greeted += [ring("slabs", n_slabs, o) for o in (-1, 1)]
    greeted += [ring("cols", n_cols, o) for o in (-1, 1)]
    greeted += [ring("cols", n_cols, o) for o in range(1, n_cols)]
    for device in greeted:
        pl.semaphore_signal(barrier, inc=1, device_id=device, device_id_type=MESH)
    pl.semaphore_wait(barrier, len(greeted))

    groups = ((1, 1), (2, J - 2), (J, 1))

    def remote(src, dst, send, recv, device):
        return pltpu.make_async_remote_copy(
            src_ref=src, dst_ref=dst, send_sem=send, recv_sem=recv,
            device_id=device, device_id_type=MESH)

    def j_copy(side, b, src=None):
        mine, theirs = ((1, J + 1), (J, 0))[side]
        if src is None:
            src = X.at[b, mine, pl.ds(1, I), inner, :]
        return remote(src, X.at[b, theirs, pl.ds(1, I), inner, :],
                      js.at[side, b], jr.at[side, b], ring("rows", n_rows, (-1, 1)[side]))

    def i_copy(side, g, b):
        mine, theirs = ((1, I + 1), (I, 0))[side]
        first, size = groups[g]
        return remote(X.at[b, pl.ds(first, size), mine, inner, :],
                      X.at[b, pl.ds(first, size), theirs, inner, :],
                      is_.at[side, g, b], ir.at[side, g, b], ring("cols", n_cols, (-1, 1)[side]))

    def k_copy(side, g, b):
        first, size = groups[g]
        return remote(KS.at[b, side, pl.ds(first - 1, size)],
                      KR.at[b, 1 - side, pl.ds(first - 1, size)],
                      ks.at[side, g, b], kr.at[side, g, b], ring("slabs", n_slabs, (-1, 1)[side]))

    def t_copy(offset, g):
        first, size = groups[g]
        return remote(TS.at[pl.ds(first - 1, size)], TR.at[offset - 1, pl.ds(first - 1, size)],
                      ts.at[offset - 1, g], tr.at[offset - 1, g], ring("cols", n_cols, offset))

    ik = lambda g, b: [k_copy(s, g, b) for s in (0, 1)] + [i_copy(s, g, b) for s in (0, 1)]

    def over(g, body):
        first, size = groups[g]

        def at(n, carry):
            body(first + n // I, 1 + n % I)
            return carry

        lax.fori_loop(0, size * I, at, 0)

    def pack(b, j, i, low, high):
        KS[b, 0, j - 1, pl.ds(i - 1, 1), :] = low
        KS[b, 1, j - 1, pl.ds(i - 1, 1), :] = high

    def update(b, g, last):
        nb = 1 - b

        def unpack(j, i):
            X[b, j, i, PAD - 1:PAD, :] = KR[b, 0, j - 1, pl.ds(i - 1, 1), :]
            X[b, j, i, PAD + K:PAD + K + 1, :] = KR[b, 1, j - 1, pl.ds(i - 1, 1), :]

        over(g, unpack)

        def cell(j, i):
            c = X[b, j, i, PAD:PAD + K, :]
            around = X[b, j, i, PAD - 1:PAD + K - 1, :] + X[b, j, i, PAD + 1:PAD + K + 1, :]
            around += X[b, j - 1, i, PAD:PAD + K, :] + X[b, j + 1, i, PAD:PAD + K, :]
            around += X[b, j, i - 1, PAD:PAD + K, :] + X[b, j, i + 1, PAD:PAD + K, :]
            c2 = c * 0.2
            new = 0.1 * around + (c * 0.4 + c2 * (1.0 - c * C[j - 1, i - 1]))
            X[nb, j, i, PAD:PAD + K, :] = new
            if not last:
                pack(nb, j, i, new[:1], new[K - 1:])

        over(g, cell)

    sent_j = {}
    sent_j[0, 0] = j_copy(0, 0, dens.at[0])
    sent_j[0, 0].start()
    load_d.wait()
    for g in range(3):
        over(g, lambda j, i: pack(0, j, i, X[0, j, i, PAD:PAD + 1, :], X[0, j, i, PAD + K - 1:PAD + K, :]))
    sent = {}
    for g in (1, 0, 2):
        sent[0, g] = ik(g, 0)
        for copy in sent[0, g]:
            copy.start()
    sent_j[0, 1] = j_copy(1, 0, dens.at[J - 1])
    sent_j[0, 1].start()
    load_c.wait()

    writes = []
    for t in range(STEPS):
        b, nb, last = t % 2, 1 - t % 2, t == STEPS - 1
        for g in (1, 0, 2):
            for copy in sent[t, g]:
                copy.wait_recv()
            if g != 1:
                side = g // 2
                sent_j[t, 1 - side].wait_recv()
            if t >= 1:
                for copy in sent[t - 1, g]:
                    copy.wait_send()
                if g != 1:
                    sent_j[t - 1, g // 2].wait_send()
            update(b, g, last)
            if not last:
                sent[t + 1, g] = ik(g, nb)
                for copy in sent[t + 1, g]:
                    copy.start()
                if g != 1:
                    sent_j[t + 1, g // 2] = j_copy(g // 2, nb)
                    sent_j[t + 1, g // 2].start()
                continue
            first, size = groups[g]
            write = pltpu.make_async_copy(
                X.at[nb, pl.ds(first, size), pl.ds(1, I), inner, :],
                end_out.at[pl.ds(first - 1, size)], ls.at[2 + g])
            write.start()
            writes.append(write)

            def total(n, carry, first=first):
                j = first + n
                so_far = X[nb, j, 1, PAD:PAD + K, :]
                for i in range(2, I + 1):
                    so_far += X[nb, j, i, PAD:PAD + K, :]
                TS[j - 1] = so_far
                return carry

            lax.fori_loop(0, size, total, 0)
            copies = [t_copy(o, g) for o in range(1, n_cols)]
            for copy in copies:
                copy.start()
            for copy in copies:
                copy.wait()
            me = lax.axis_index("cols")

            def running(n, carry, first=first):
                j = first + n
                so_far = jnp.zeros((K, S), jnp.float32)
                for o in range(1, n_cols):
                    so_far += jnp.where(o <= me, TR[o - 1, j - 1], 0.0)
                for i in range(1, I + 1):
                    so_far += X[nb, j, i, PAD:PAD + K, :]
                    PT[j - 1, i - 1] = so_far * (1.0 / cells)
                return carry

            lax.fori_loop(0, size, running, 0)
            write = pltpu.make_async_copy(
                PT.at[pl.ds(first - 1, size)], pot_out.at[pl.ds(first - 1, size)], ls.at[5 + g])
            write.start()
            writes.append(write)
    for g in range(3):
        for copy in sent[STEPS - 1, g]:
            copy.wait_send()
    for side in range(2):
        sent_j[STEPS - 1, side].wait_send()
    for write in writes:
        write.wait()


def solution(mesh):
    counts = tuple(mesh.shape[axis] for axis in ("rows", "cols", "slabs"))

    def per_device(density, crowding):
        J, I, K, S = density.shape
        n_cols = counts[1]
        any_space = pl.BlockSpec(memory_space=pl.ANY)
        dma = pltpu.SemaphoreType.DMA
        return pl.pallas_call(
            functools.partial(kernel, density.shape, counts),
            out_shape=[jax.ShapeDtypeStruct(density.shape, density.dtype)] * 2,
            in_specs=[any_space] * 2,
            out_specs=[any_space] * 2,
            scratch_shapes=[
                pltpu.VMEM((2, J + 2, I + 2, K + 2 * PAD, S), jnp.float32),
                pltpu.VMEM((J, I, K, S), jnp.float32),
                pltpu.VMEM((J, I, K, S), jnp.float32),
                pltpu.VMEM((2, 2, J, I, S), jnp.float32),
                pltpu.VMEM((2, 2, J, I, S), jnp.float32),
                pltpu.VMEM((J, K, S), jnp.float32),
                pltpu.VMEM((n_cols - 1, J, K, S), jnp.float32),
                dma((2, 2)), dma((2, 2)),
                dma((2, 3, 2)), dma((2, 3, 2)),
                dma((2, 3, 2)), dma((2, 3, 2)),
                dma((n_cols - 1, 3)), dma((n_cols - 1, 3)),
                dma((8,)),
            ],
            compiler_params=pltpu.CompilerParams(
                collective_id=0, has_side_effects=True, vmem_limit_bytes=56 * 2**20),
            name="reaction_diffusion",
        )(density, crowding)

    spec = P(("copy", "rows"), "cols", "slabs", None)
    return jax.shard_map(
        per_device, mesh=mesh, in_specs=(spec, spec), out_specs=(spec, spec), check_vma=False)
```

time: 354 us -> 153 us (0.43)
  waiting for transfers between devices: 191 us -> 0 us
  Pallas kernels: 0 us -> 145 us
  other arithmetic: 101 us -> 0 us
  starting transfers between devices: 35.5 us -> 0 us
  between operations: 14.4 us -> 0.65 us
  local copies, waits for them, and re-layouts: 11.6 us -> 6.96 us
    ppermute x36 -> x0, waiting for transfers between devices: 181 us -> none  [the longest x18 140 us: padded_2(): before = lax.ppermute(last, axis, up)]
    pallas_call x0 -> x1, Pallas kernels: none -> 145 us  [per_device(): pl.pallas_call(functools.partial(kernel, density.shape, counts), out_shap...]
    add x6 -> x0, other arithmetic: 87.5 us -> none  [one_step(): return middle + 0.1 * spread + 0.2 * middle * (1.0 - middle * crowding)]
    ppermute x36 -> x0, starting transfers between devices: 35.5 us -> none  [the longest x18 21.4 us: padded_2(): before = lax.ppermute(last, axis, up)]
    all_gather x1 -> x0, waiting for transfers between devices: 10.4 us -> none  [carried_in(): pieces = lax.all_gather(value, axis)]
    slice x20 -> x0, local copies, waits for them, and re-layouts: 5.87 us -> none  [the longest x12 3.9 us: padded_2(): last = lax.slice_in_dim(shard, length - width, length, axis=dim)]
    div x1 -> x0, other arithmetic: 5.18 us -> none  [per_device(): potential = (here + below) / (density.shape[1] * lax.axis_size('cols'))]
    slice x11 -> x0, other arithmetic: 4.84 us -> none  [padded_2(): last = lax.slice_in_dim(shard, length - width, length, axis=dim)]
  transfers between devices with their start and end apart: 37 -> 0, of which waited for: 37 -> 0; matrix products, arithmetic and copies ran while one was open for 1% -> 0% of each run, Pallas kernels for 0% -> 0%
where the time goes in v1:
time: 153 us
  Pallas kernels  145 us (95%)
  local copies, waits for them, and re-layouts  6.96 us (5%)
    pallas_call x1, Pallas kernels, per_device(): pl.pallas_call(functools.partial(kernel, density.shape, counts), out_shap...  145 us
    unnamed x4, local copies, waits for them, and re-layouts  6.96 us

profile of v1, /device:TPU:0, one launch (start us, length us, event | category | flops | bytes accessed | tf_op | source)
XLA Modules:
  0.0 152.9 jit_solution(3418262217894675275)
XLA Ops:
  0.6 145.3 %reaction_diffusion.1 = (f32[16,8,64,128]{3,2,1,0:T(8,128)}, f32[16,8,64,128]{3,2,1,0:T(8,128)}) custom-call(f32[16,8,64,128]{3,2,1,0:T(8,128)} %dens.1, f32[16,8,64,128]{3,2,1,0:T(8,128)} %crow.1), custom_call_target="tpu_custom_call" | custom-call | tf_op jit(solution)/shard_map/reaction_diffusion/pallas_call | solution.py:201
  145.9 0.0 copy-start
  145.9 4.9 %copy.6 = f32[16,8,64,128]{3,2,1,0:T(8,128)} copy(f32[16,8,64,128]{3,2,1,0:T(8,128)} %get-tuple-element.4) | data formatting | bytes 8388608
  150.8 0.0 copy-done
  150.8 2.0 %copy.7 = f32[16,8,64,128]{3,2,1,0:T(8,128)} copy(f32[16,8,64,128]{3,2,1,0:T(8,128)S(1)} %copy-done) | data formatting | bytes 8388608
Async XLA Ops:
  145.9 5.0 %copy-start = (f32[16,8,64,128]{3,2,1,0:T(8,128)S(1)}, f32[16,8,64,128]{3,2,1,0:T(8,128)}, u32[]{:S(2)}) copy-start(f32[16,8,64,128]{3,2,1,0:T(8,128)} %get-tuple-element.5) | copy-start | bytes 12582916

commit v2 on v1

v2 whole, which is shorter than its diff:
```python
import functools

import jax
import jax.numpy as jnp
from jax import lax
from jax.experimental import pallas as pl
from jax.experimental.pallas import tpu as pltpu
from jax.sharding import PartitionSpec as P

STEPS = 6
MESH = pl.DeviceIdType.MESH
VMEM_FIRST = 47 * 2**20
VMEM_SECOND = 20 * 2**20
PAD = 8


def kernel(shape, counts, dens, crow, end, below, X0, X1, C, KS, KR, TS, TR,
           js, jr, is_, ir, ks, kr, ts, tr, ls):
    J, I, K, S = shape
    n_rows, n_cols, n_slabs = counts
    X = (X0, X1)
    inner = pl.ds(PAD, K)

    def ring(axis, count, offset):
        return {axis: lax.rem(lax.axis_index(axis) + (offset + count), count)}

    load_d = pltpu.make_async_copy(dens, X0.at[pl.ds(1, J), pl.ds(1, I), inner, :], ls.at[0])
    load_c = pltpu.make_async_copy(crow, C, ls.at[1])
    load_d.start()
    load_c.start()

    barrier = pltpu.get_barrier_semaphore()
    greeted = [ring("rows", n_rows, o) for o in (-1, 1)]
    greeted += [ring("slabs", n_slabs, o) for o in (-1, 1)]
    greeted += [ring("cols", n_cols, o) for o in (-1, 1)]
    greeted += [ring("cols", n_cols, o) for o in range(1, n_cols)]
    for device in greeted:
        pl.semaphore_signal(barrier, inc=1, device_id=device, device_id_type=MESH)

    groups = ((1, 1), (2, J - 2), (J, 1))

    def remote(src, dst, send, recv, device):
        return pltpu.make_async_remote_copy(
            src_ref=src, dst_ref=dst, send_sem=send, recv_sem=recv,
            device_id=device, device_id_type=MESH)

    def j_copy(side, b, src=None):
        mine, theirs = ((1, J + 1), (J, 0))[side]
        if src is None:
            src = X[b].at[mine, pl.ds(1, I), inner, :]
        return remote(src, X[b].at[theirs, pl.ds(1, I), inner, :],
                      js.at[side, b], jr.at[side, b], ring("rows", n_rows, (-1, 1)[side]))

    def i_copy(side, g, b):
        mine, theirs = ((1, I + 1), (I, 0))[side]
        first, size = groups[g]
        return remote(X[b].at[pl.ds(first, size), mine, inner, :],
                      X[b].at[pl.ds(first, size), theirs, inner, :],
                      is_.at[side, g, b], ir.at[side, g, b], ring("cols", n_cols, (-1, 1)[side]))

    def k_copy(side, g, b):
        first, size = groups[g]
        return remote(KS.at[b, side, pl.ds(first - 1, size)],
                      KR.at[b, 1 - side, pl.ds(first - 1, size)],
                      ks.at[side, g, b], kr.at[side, g, b], ring("slabs", n_slabs, (-1, 1)[side]))

    def t_copy(offset, g):
        first, size = groups[g]
        return remote(TS.at[pl.ds(first - 1, size)], TR.at[offset - 1, pl.ds(first - 1, size)],
                      ts.at[offset - 1, g], tr.at[offset - 1, g], ring("cols", n_cols, offset))

    ik = lambda g, b: [k_copy(s, g, b) for s in (0, 1)] + [i_copy(s, g, b) for s in (0, 1)]

    def over(g, body):
        first, size = groups[g]

        def at(n, carry):
            for i in range(1, I + 1):
                body(first + n, i)
            return carry

        lax.fori_loop(0, size, at, 0)

    def pack(b, j, i, low, high):
        KS[b, 0, j - 1, pl.ds(i - 1, 1), :] = low
        KS[b, 1, j - 1, pl.ds(i - 1, 1), :] = high

    def update(b, g, last):
        nb = 1 - b

        def unpack(j, i):
            X[b][j, i, PAD - 1:PAD, :] = KR[b, 0, j - 1, pl.ds(i - 1, 1), :]
            X[b][j, i, PAD + K:PAD + K + 1, :] = KR[b, 1, j - 1, pl.ds(i - 1, 1), :]

        over(g, unpack)

        def cell(j, i):
            c = X[b][j, i, PAD:PAD + K, :]
            around = X[b][j, i, PAD - 1:PAD + K - 1, :] + X[b][j, i, PAD + 1:PAD + K + 1, :]
            around += X[b][j - 1, i, PAD:PAD + K, :] + X[b][j + 1, i, PAD:PAD + K, :]
            around += X[b][j, i - 1, PAD:PAD + K, :] + X[b][j, i + 1, PAD:PAD + K, :]
            c2 = c * 0.2
            new = 0.1 * around + (c * 0.4 + c2 * (1.0 - c * C[j - 1, i - 1]))
            if last:
                end[j - 1, i - 1] = new
            else:
                X[nb][j, i, PAD:PAD + K, :] = new
                pack(nb, j, i, new[:1], new[K - 1:])

        over(g, cell)

    load_d.wait()
    for g in range(3):
        over(g, lambda j, i: pack(0, j, i, X0[j, i, PAD:PAD + 1, :], X0[j, i, PAD + K - 1:PAD + K, :]))
    pl.semaphore_wait(barrier, len(greeted))
    sent, sent_j = {}, {}
    for g in (1, 0, 2):
        sent[0, g] = ik(g, 0)
        for copy in sent[0, g]:
            copy.start()
    for side in (0, 1):
        sent_j[0, side] = j_copy(side, 0, (dens.at[0], dens.at[J - 1])[side])
    sent_j[0, 0].start()
    load_c.wait()

    me = lax.axis_index("cols")
    totals = []
    for t in range(STEPS):
        b, nb, last = t % 2, 1 - t % 2, t == STEPS - 1
        for g in (1, 0, 2):
            for copy in sent[t, g]:
                copy.wait_recv()
            if g != 1:
                sent_j[t, 1 - g // 2].wait_recv()
            if t >= 1:
                for copy in sent[t - 1, g]:
                    copy.wait_send()
                if g != 1:
                    sent_j[t - 1, g // 2].wait_send()
            update(b, g, last)
            if not last:
                sent[t + 1, g] = ik(g, nb)
                for copy in sent[t + 1, g]:
                    copy.start()
                if g != 1:
                    sent_j[t + 1, g // 2] = j_copy(g // 2, nb)
            if g == 1:
                sent_j[t, 1].start()
            elif g == 0 and not last:
                sent_j[t + 1, 0].start()
            if not last:
                continue
            first, size = groups[g]

            def total(n, carry, first=first):
                j = first + n
                so_far = end[j - 1, 0]
                for i in range(1, I):
                    so_far += end[j - 1, i]
                TS[j - 1] = so_far
                return carry

            lax.fori_loop(0, size, total, 0)
            copies = [t_copy(o, g) for o in range(1, n_cols)]
            for copy in copies:
                copy.start()
            totals.append((g, copies))
    for g, copies in totals:
        first, size = groups[g]
        for copy in copies:
            copy.wait()

        def gather(n, carry, first=first):
            j = first + n
            so_far = jnp.zeros((K, S), jnp.float32)
            for o in range(1, n_cols):
                so_far += jnp.where(o <= me, TR[o - 1, j - 1], 0.0)
            below[j - 1] = so_far
            return carry

        lax.fori_loop(0, size, gather, 0)
    for g in range(3):
        for copy in sent[STEPS - 1, g]:
            copy.wait_send()
    for side in range(2):
        sent_j[STEPS - 1, side].wait_send()


def write_out(cells, end, below, pot_out, end_out, PT, sems):
    J, I, K, S = end.shape
    parts = 4 if J % 4 == 0 else 1
    size = J // parts
    writes = []
    for p in range(parts):
        here = pl.ds(p * size, size)
        writes.append(pltpu.make_async_copy(end.at[here], end_out.at[here], sems.at[0, p]))
        writes[-1].start()
    for p in range(parts):
        def running(n, carry, p=p):
            j = p * size + n
            so_far = below[j]
            for i in range(I):
                so_far += end[j, i]
                PT[j, i] = so_far * (1.0 / cells)
            return carry

        lax.fori_loop(0, size, running, 0)
        here = pl.ds(p * size, size)
        writes.append(pltpu.make_async_copy(PT.at[here], pot_out.at[here], sems.at[1, p]))
        writes[-1].start()
    for write in writes:
        write.wait()


def solution(mesh):
    counts = tuple(mesh.shape[axis] for axis in ("rows", "cols", "slabs"))

    def per_device(density, crowding):
        J, I, K, S = density.shape
        n_cols = counts[1]
        any_space = pl.BlockSpec(memory_space=pl.ANY)
        dma = pltpu.SemaphoreType.DMA
        vmem = pl.BlockSpec(memory_space=pltpu.VMEM)
        padded = pltpu.VMEM((J + 2, I + 2, K + 2 * PAD, S), jnp.float32)
        end, below = pl.pallas_call(
            functools.partial(kernel, density.shape, counts),
            out_shape=[jax.ShapeDtypeStruct((J, I, K, S), jnp.float32),
                       jax.ShapeDtypeStruct((J, K, S), jnp.float32)],
            in_specs=[any_space] * 2,
            out_specs=[vmem] * 2,
            scratch_shapes=[
                padded, padded,
                pltpu.VMEM((J, I, K, S), jnp.float32),
                pltpu.VMEM((2, 2, J, I, S), jnp.float32),
                pltpu.VMEM((2, 2, J, I, S), jnp.float32),
                pltpu.VMEM((J, K, S), jnp.float32),
                pltpu.VMEM((n_cols - 1, J, K, S), jnp.float32),
                dma((2, 2)), dma((2, 2)),
                dma((2, 3, 2)), dma((2, 3, 2)),
                dma((2, 3, 2)), dma((2, 3, 2)),
                dma((n_cols - 1, 3)), dma((n_cols - 1, 3)),
                dma((2,)),
            ],
            compiler_params=pltpu.CompilerParams(
                collective_id=0, has_side_effects=True, vmem_limit_bytes=VMEM_FIRST),
            name="reaction_diffusion",
        )(density, crowding)
        return pl.pallas_call(
            functools.partial(write_out, I * n_cols),
            out_shape=[jax.ShapeDtypeStruct(density.shape, density.dtype)] * 2,
            in_specs=[vmem] * 2,
            out_specs=[any_space] * 2,
            scratch_shapes=[pltpu.VMEM((J, I, K, S), jnp.float32), dma((2, 4))],
            compiler_params=pltpu.CompilerParams(vmem_limit_bytes=VMEM_SECOND),
            name="write_out",
        )(end, below)

    spec = P(("copy", "rows"), "cols", "slabs", None)
    return jax.shard_map(
        per_device, mesh=mesh, in_specs=(spec, spec), out_specs=(spec, spec), check_vma=False)
```

time: 153 us -> 148 us (0.967)
  local copies, waits for them, and re-layouts: 6.96 us -> 0 us
  Pallas kernels: 145 us -> 148 us
    unnamed x4 -> x0, local copies, waits for them, and re-layouts: 6.96 us -> none
    pallas_call x0 -> x1, Pallas kernels: none -> 3.37 us  [per_device(): pl.pallas_call(functools.partial(write_out, I * n_cols), out_shape=[jax.S...]
where the time goes in v2:
time: 148 us
  Pallas kernels  148 us (100%)
    pallas_call x1, Pallas kernels, per_device(): pl.pallas_call(functools.partial(kernel, density.shape, counts), out_shap...  144 us
    pallas_call x1, Pallas kernels, per_device(): pl.pallas_call(functools.partial(write_out, I * n_cols), out_shape=[jax.S...  3.37 us

profile of v2, /device:TPU:0, one launch (start us, length us, event | category | flops | bytes accessed | tf_op | source)
XLA Modules:
  0.0 148.2 jit_solution(17901523087535428229)
XLA Ops:
  0.6 144.2 %reaction_diffusion.1 = (f32[16,8,64,128]{3,2,1,0:T(8,128)S(1)}, f32[16,64,128]{2,1,0:T(8,128)S(1)}) custom-call(f32[16,8,64,128]{3,2,1,0:T(8,128)} %dens.1, f32[16,8,64,128]{3,2,1,0:T(8,128)} %crow.1), custom_call_target="tpu_custom_call" | custom-call | tf_op jit(solution)/shard_map/reaction_diffusion/pallas_call | solution.py:225
  144.9 3.4 %write_out.1 = (f32[16,8,64,128]{3,2,1,0:T(8,128)}, f32[16,8,64,128]{3,2,1,0:T(8,128)}) custom-call(f32[16,8,64,128]{3,2,1,0:T(8,128)S(1)} %get-tuple-element.4.end, f32[16,64,128]{2,1,0:T(8,128)S(1)} %get-tuple-element.5.below), custom_call_target="tpu_custom_call" | custom-call | tf_op jit(solution)/shard_map/write_out/pallas_call | solution.py:248

commit v3 on v2

--- a/solution.py
+++ b/solution.py
@@ -27,7 +27,6 @@
     load_d = pltpu.make_async_copy(dens, X0.at[pl.ds(1, J), pl.ds(1, I), inner, :], ls.at[0])
     load_c = pltpu.make_async_copy(crow, C, ls.at[1])
     load_d.start()
-    load_c.start()
 
     barrier = pltpu.get_barrier_semaphore()
     greeted = [ring("rows", n_rows, o) for o in (-1, 1)]
@@ -44,11 +43,9 @@
             src_ref=src, dst_ref=dst, send_sem=send, recv_sem=recv,
             device_id=device, device_id_type=MESH)
 
-    def j_copy(side, b, src=None):
+    def j_copy(side, b):
         mine, theirs = ((1, J + 1), (J, 0))[side]
-        if src is None:
-            src = X[b].at[mine, pl.ds(1, I), inner, :]
-        return remote(src, X[b].at[theirs, pl.ds(1, I), inner, :],
+        return remote(X[b].at[mine, pl.ds(1, I), inner, :], X[b].at[theirs, pl.ds(1, I), inner, :],
                       js.at[side, b], jr.at[side, b], ring("rows", n_rows, (-1, 1)[side]))
 
     def i_copy(side, g, b):
@@ -85,14 +82,15 @@
         KS[b, 0, j - 1, pl.ds(i - 1, 1), :] = low
         KS[b, 1, j - 1, pl.ds(i - 1, 1), :] = high
 
+    def unpack(b, g):
+        def cell(j, i):
+            X[b][j, i, PAD - 1:PAD, :] = KR[b, 0, j - 1, pl.ds(i - 1, 1), :]
+            X[b][j, i, PAD + K:PAD + K + 1, :] = KR[b, 1, j - 1, pl.ds(i - 1, 1), :]
+
+        over(g, cell)
+
     def update(b, g, last):
         nb = 1 - b
-
-        def unpack(j, i):
-            X[b][j, i, PAD - 1:PAD, :] = KR[b, 0, j - 1, pl.ds(i - 1, 1), :]
-            X[b][j, i, PAD + K:PAD + K + 1, :] = KR[b, 1, j - 1, pl.ds(i - 1, 1), :]
-
-        over(g, unpack)
 
         def cell(j, i):
             c = X[b][j, i, PAD:PAD + K, :]
@@ -110,26 +108,50 @@
         over(g, cell)
 
     load_d.wait()
+    load_c.start()
     for g in range(3):
         over(g, lambda j, i: pack(0, j, i, X0[j, i, PAD:PAD + 1, :], X0[j, i, PAD + K - 1:PAD + K, :]))
     pl.semaphore_wait(barrier, len(greeted))
     sent, sent_j = {}, {}
+    for side in (0, 1):
+        sent_j[0, side] = j_copy(side, 0)
     for g in (1, 0, 2):
         sent[0, g] = ik(g, 0)
-        for copy in sent[0, g]:
+        for copy in sent[0, g][:2]:
             copy.start()
-    for side in (0, 1):
-        sent_j[0, side] = j_copy(side, 0, (dens.at[0], dens.at[J - 1])[side])
     sent_j[0, 0].start()
+    for g in (1, 0, 2):
+        for copy in sent[0, g][2:]:
+            copy.start()
     load_c.wait()
 
     me = lax.axis_index("cols")
     totals = []
+
+    def collect(g, copies):
+        first, size = groups[g]
+        for copy in copies:
+            copy.wait()
+
+        def gather(n, carry):
+            j = first + n
+            so_far = jnp.zeros((K, S), jnp.float32)
+            for o in range(1, n_cols):
+                so_far += jnp.where(o <= me, TR[o - 1, j - 1], 0.0)
+            below[j - 1] = so_far
+            return carry
+
+        lax.fori_loop(0, size, gather, 0)
+
     for t in range(STEPS):
         b, nb, last = t % 2, 1 - t % 2, t == STEPS - 1
         for g in (1, 0, 2):
             for copy in sent[t, g]:
                 copy.wait_recv()
+            unpack(b, g)
+            if last and g == 2:
+                for earlier in totals:
+                    collect(*earlier)
             if g != 1:
                 sent_j[t, 1 - g // 2].wait_recv()
             if t >= 1:
@@ -165,20 +187,7 @@
             for copy in copies:
                 copy.start()
             totals.append((g, copies))
-    for g, copies in totals:
-        first, size = groups[g]
-        for copy in copies:
-            copy.wait()
-
-        def gather(n, carry, first=first):
-            j = first + n
-            so_far = jnp.zeros((K, S), jnp.float32)
-            for o in range(1, n_cols):
-                so_far += jnp.where(o <= me, TR[o - 1, j - 1], 0.0)
-            below[j - 1] = so_far
-            return carry
-
-        lax.fori_loop(0, size, gather, 0)
+    collect(*totals[2])
     for g in range(3):
         for copy in sent[STEPS - 1, g]:
             copy.wait_send()

time: 148 us -> 149 us (level)
  no operation moved by 1% of the time
where the time goes in v3:
time: 149 us
  Pallas kernels  148 us (99%)
    pallas_call x1, Pallas kernels, per_device(): pl.pallas_call(functools.partial(kernel, density.shape, counts), out_shap...  145 us
    pallas_call x1, Pallas kernels, per_device(): pl.pallas_call(functools.partial(write_out, I * n_cols), out_shape=[jax.S...  3.37 us

profile of v3, /device:TPU:0, one launch (start us, length us, event | category | flops | bytes accessed | tf_op | source)
XLA Modules:
  0.0 149.0 jit_solution(7743742640930238042)
XLA Ops:
  0.6 145.0 %reaction_diffusion.1 = (f32[16,8,64,128]{3,2,1,0:T(8,128)S(1)}, f32[16,64,128]{2,1,0:T(8,128)S(1)}) custom-call(f32[16,8,64,128]{3,2,1,0:T(8,128)} %dens.1, f32[16,8,64,128]{3,2,1,0:T(8,128)} %crow.1), custom_call_target="tpu_custom_call" | custom-call | tf_op jit(solution)/shard_map/reaction_diffusion/pallas_call | solution.py:234
  145.7 3.4 %write_out.1 = (f32[16,8,64,128]{3,2,1,0:T(8,128)}, f32[16,8,64,128]{3,2,1,0:T(8,128)}) custom-call(f32[16,8,64,128]{3,2,1,0:T(8,128)S(1)} %get-tuple-element.4.end, f32[16,64,128]{2,1,0:T(8,128)S(1)} %get-tuple-element.5.below), custom_call_target="tpu_custom_call" | custom-call | tf_op jit(solution)/shard_map/write_out/pallas_call | solution.py:257
